TPU v7x, 32 devices: a whole 2x2x4 slice. The times are simulated.
32 devices in a mesh: tok: 2 (over x), vocab: 16 (over z, y, core).
Axes of the slice: x: 2, y: 2, z: 4, core: 2. Of those that a mesh axis runs over, the one named last changes fastest.
Arguments:
- hidden: bfloat16 [1536, 4096], P('tok', 'vocab'), as said below
- weight: bfloat16 [4096, 16384], P('tok', 'vocab'), may hold values from -0.09375 to 0.09375
- targets: int32 [1536], P('tok'), may hold values from 0 to 16383
- domains: int32 [1536], P('tok'), may hold values from 0 to 63
- seq_len: int32 [12], P('tok'), may hold values from 1 to 128
Outputs:
- token_loss: float32 [1536], P(('tok', 'vocab'))
- domain_mean: float32 [64], replicated
Inputs may be any that keep to these rules, and one draw needn't show every extreme that they name: hidden states of the eval window.
All inputs are finite; a program needn't handle non-finite values.
Results may differ from a plain program's by a relative error of at most 0.0003.
Values may be sent and summed in bfloat16 or wider, within the bound.
A program may use at most 64 MiB of HBM per device.

v0:
```python
import jax
import jax.numpy as jnp
from jax import lax
from jax.sharding import PartitionSpec as P

SEQ_LEN = 128
DOMAINS = 64


def body(hidden, weight, targets, domains, seq_len):
    features = lax.all_gather(hidden, "vocab", axis=1, tiled=True)
    tok_rows = features.shape[0]
    columns = weight.shape[1]
    logits = jnp.dot(
        features,
        lax.all_gather(weight, "tok", axis=0, tiled=True),
        preferred_element_type=jnp.float32,
    )
    first_col = lax.axis_index("vocab") * columns
    column_ids = first_col + lax.broadcasted_iota(jnp.int32, (tok_rows, columns), 1)
    picked_loc = jnp.sum(jnp.where(column_ids == targets[:, None], logits, 0.0), axis=1)
    top_loc = jnp.max(logits, axis=1)
    groups = lax.axis_size("vocab")
    share_len = tok_rows // groups
    share_start = lax.axis_index("vocab") * share_len
    sum_loc = jnp.sum(jnp.exp(logits - top_loc[:, None]), axis=1)
    gathered = (
        lax.all_to_all(
            top_loc.reshape(groups, share_len), "vocab", split_axis=0, concat_axis=0, tiled=True
        ),
        lax.all_to_all(
            sum_loc.reshape(groups, share_len), "vocab", split_axis=0, concat_axis=0, tiled=True
        ),
        lax.all_to_all(
            picked_loc.reshape(groups, share_len), "vocab", split_axis=0, concat_axis=0, tiled=True
        ),
    )
    row_top = jnp.max(gathered[0], axis=0)
    row_total = jnp.sum(gathered[1] * jnp.exp(gathered[0] - row_top[None, :]), axis=0)
    picked = jnp.sum(gathered[2], axis=0)
    loss_raw = jnp.log(row_total) + row_top - picked
    positions = share_start + lax.iota(jnp.int32, share_len)
    seq_ids = positions // SEQ_LEN
    seq_count = seq_len.shape[0]
    lengths = jnp.sum(
        jnp.where(
            seq_ids[:, None] == lax.broadcasted_iota(jnp.int32, (share_len, seq_count), 1),
            seq_len[None, :],
            0,
        ),
        axis=1,
    )
    valid_mask = (positions % SEQ_LEN < lengths).astype(jnp.float32)
    token_loss = loss_raw * valid_mask
    domain_share = lax.dynamic_slice_in_dim(domains, share_start, share_len)
    onehot = (
        domain_share[:, None] == lax.broadcasted_iota(jnp.int32, (share_len, DOMAINS), 1)
    ).astype(jnp.float32)
    domain_sum = jnp.dot(token_loss, onehot, precision=lax.Precision.HIGHEST)
    domain_count = jnp.dot(valid_mask, onehot, precision=lax.Precision.HIGHEST)
    domain_sum, domain_count = lax.psum((domain_sum, domain_count), ("tok", "vocab"))
    domain_mean = domain_sum / jnp.maximum(domain_count, 1.0)
    return (token_loss, domain_mean)


def solution(mesh):
    in_specs = (P("tok", "vocab"), P("tok", "vocab"), P("tok"), P("tok"), P("tok"))
    out_specs = (P(("tok", "vocab")), P())
    return jax.shard_map(body, mesh=mesh, in_specs=in_specs, out_specs=out_specs, check_vma=False)
```

profile of v0, /device:TPU:0, one launch (start us, length us, event | category | flops | bytes accessed | tf_op | source)
XLA Modules:
  0.0 270.7 jit_solution(16608660790201364310)
XLA Ops:
  7.2 0.0 all-gather.5.cloned.1.call-start
  7.2 0.7 all-gather.5.cloned.1.call-update
  7.9 0.0 all-gather.3.cloned.1.call-start
  7.9 0.7 all-gather.3.cloned.1.call-update
  8.7 0.0 copy-start
  8.7 107.6 %all-gather.5.cloned.1.call-done = bf16[4096,1024]{1,0:T(8,128)(2,1)} async-done(((bf16[2048,1024]{1,0:T(8,128)(2,1)}), bf16[4096,1024]{1,0:T(8,128)(2,1)}) %all-gather.5.cloned.1.call-update) | async-done | bytes 8388624 | tf_op jit(solution)/shard_map/all_gather | solution.py:16
  116.2 67.4 %all-gather.3.cloned.1.call-done = bf16[768,4096]{1,0:T(8,128)(2,1)} async-done(((bf16[768,256]{1,0:T(8,128)(2,1)}), bf16[768,4096]{1,0:T(8,128)(2,1)}) %all-gather.3.cloned.1.call-update) | async-done | bytes 6291472 | tf_op jit(solution)/shard_map/all_gather | solution.py:11
  183.7 11.1 %fusion.6 = (f32[768]{0:T(1024)S(1)}, f32[768,1024]{1,0:T(8,128)S(1)}) fusion(bf16[768,4096]{1,0:T(8,128)(2,1)} %all-gather.3.cloned.1.call-done, bf16[4096,1024]{1,0:T(8,128)(2,1)} %all-gather.5.cloned.1.call-done), kind=kOutput, calls=%fused_computation.22 | convolution fusion | flops 6443236352 | bytes 17828864 | tf_op jit(solution)/shard_map/dot_general | solution.py:14
  194.8 0.0 copy-start.2
  194.8 0.7 all_to_all.25
  195.4 3.4 %all-to-all-start.1 = ((f32[16,1,48]{2,1,0:T(1,128)}), f32[16,1,48]{2,1,0:T(1,128)S(1)}, u32[]{:S(2)}, u32[]{:S(2)}) async-start(f32[16,1,48]{2,1,0:T(1,128)} %all_to_all.25), calls=%async_computation.1 | async-start | bytes 16384 | tf_op jit(solution)/shard_map/all_to_all | solution.py:28
  198.9 0.0 copy-done
  198.9 0.9 exponential_reduce_fusion
  199.8 0.7 all_to_all.28
  200.5 4.8 %all-to-all-done.1 = f32[16,1,48]{2,1,0:T(1,128)S(1)} async-done(((f32[16,1,48]{2,1,0:T(1,128)}), f32[16,1,48]{2,1,0:T(1,128)S(1)}, u32[]{:S(2)}, u32[]{:S(2)}) %all-to-all-start.1) | async-done | bytes 3104 | tf_op jit(solution)/shard_map/all_to_all | solution.py:28
  205.3 3.5 %all-to-all-start.2 = ((f32[16,1,48]{2,1,0:T(1,128)}), f32[16,1,48]{2,1,0:T(1,128)S(1)}, u32[]{:S(2)}, u32[]{:S(2)}) async-start(f32[16,1,48]{2,1,0:T(1,128)} %all_to_all.28), calls=%async_computation.2 | async-start | bytes 16384 | tf_op jit(solution)/shard_map/all_to_all | solution.py:34
  208.8 0.0 copy-done.2
  208.8 0.1 select_reduce_fusion.1
  208.9 0.8 dynamic_slice.3
  209.6 0.7 all_to_all.22
  210.3 4.9 %all-to-all-done.2 = f32[16,1,48]{2,1,0:T(1,128)S(1)} async-done(((f32[16,1,48]{2,1,0:T(1,128)}), f32[16,1,48]{2,1,0:T(1,128)S(1)}, u32[]{:S(2)}, u32[]{:S(2)}) %all-to-all-start.2) | async-done | bytes 3104 | tf_op jit(solution)/shard_map/all_to_all | solution.py:34
  215.2 3.4 %all-to-all-start = ((f32[16,1,48]{2,1,0:T(1,128)}), f32[16,1,48]{2,1,0:T(1,128)S(1)}, u32[]{:S(2)}, u32[]{:S(2)}) async-start(f32[16,1,48]{2,1,0:T(1,128)} %all_to_all.22), calls=%async_computation | async-start | bytes 16384 | tf_op jit(solution)/shard_map/all_to_all | solution.py:31
  218.6 0.2 convolution_bitcast_fusion
  218.8 6.1 %all-to-all-done = f32[16,1,48]{2,1,0:T(1,128)S(1)} async-done(((f32[16,1,48]{2,1,0:T(1,128)}), f32[16,1,48]{2,1,0:T(1,128)S(1)}, u32[]{:S(2)}, u32[]{:S(2)}) %all-to-all-start) | async-done | bytes 3104 | tf_op jit(solution)/shard_map/all_to_all | solution.py:31
  225.0 0.0 copy-start.1
  225.0 0.2 convolution_bitcast_fusion.1
  225.2 38.2 %all-reduce = (f32[64]{0:T(128)S(1)}, f32[64]{0:T(128)S(1)}) all-reduce(f32[64]{0:T(128)S(1)} %convolution_bitcast_fusion.1, f32[64]{0:T(128)S(1)} %convolution_bitcast_fusion), channel_id=1, replica_groups=mesh['tok'=2,'vocab'=16] {'tok','vocab'}, use_global_device_ids=true, to_apply=%region_7.8 | all-reduce | flops 128 | bytes 1024 | tf_op jit(solution)/shard_map/psum | solution.py:61
  263.4 0.5 maximum_divide_fusion
  263.9 0.0 copy-done.1
  (6 shorter events, 0.1 us)
Async XLA Ops:
  7.2 109.1 %all-gather.5.cloned.1.call-start = ((), (), s32[]{:S(2)}) async-start(), calls=%async_computation.4 | async-start | bytes 12582912 | tf_op jit(solution)/shard_map/all_gather | solution.py:16
  7.9 175.8 %all-gather.3.cloned.1.call-start = ((), (), s32[]{:S(2)}) async-start(), calls=%async_computation.3 | async-start | bytes 6684672 | tf_op jit(solution)/shard_map/all_gather | solution.py:11
  8.7 190.2 %copy-start = (s32[768]{0:T(1024)S(1)}, s32[768]{0:T(1024)}, u32[]{:S(2)}) copy-start(s32[768]{0:T(1024)} %param.7) | copy-start | bytes 9220
  194.8 14.0 %copy-start.2 = (s32[6]{0:T(128)S(1)}, s32[6]{0:T(128)}, u32[]{:S(2)}) copy-start(s32[6]{0:T(128)} %param.9) | copy-start | bytes 76
  195.4 9.8 %all-to-all-start.1 = ((f32[16,1,48]{2,1,0:T(1,128)}), f32[16,1,48]{2,1,0:T(1,128)S(1)}, u32[]{:S(2)}, u32[]{:S(2)}) async-start(f32[16,1,48]{2,1,0:T(1,128)} %all_to_all.25), calls=%async_computation.1 | async-start | bytes 16384 | tf_op jit(solution)/shard_map/all_to_all | solution.py:28
  205.3 9.9 %all-to-all-start.2 = ((f32[16,1,48]{2,1,0:T(1,128)}), f32[16,1,48]{2,1,0:T(1,128)S(1)}, u32[]{:S(2)}, u32[]{:S(2)}) async-start(f32[16,1,48]{2,1,0:T(1,128)} %all_to_all.28), calls=%async_computation.2 | async-start | bytes 16384 | tf_op jit(solution)/shard_map/all_to_all | solution.py:34
  215.2 9.8 %all-to-all-start = ((f32[16,1,48]{2,1,0:T(1,128)}), f32[16,1,48]{2,1,0:T(1,128)S(1)}, u32[]{:S(2)}, u32[]{:S(2)}) async-start(f32[16,1,48]{2,1,0:T(1,128)} %all_to_all.22), calls=%async_computation | async-start | bytes 16384 | tf_op jit(solution)/shard_map/all_to_all | solution.py:31
  225.0 38.9 %copy-start.1 = (f32[48]{0:T(128)}, f32[48]{0:T(128)S(1)}, u32[]{:S(2)}) copy-start(f32[48]{0:T(128)S(1)} %subtract_select_fusion) | copy-start | bytes 580
Sparse Core Ops, SparseCore 0:
  9.5 106.6 all-gather.4
  118.4 65.2 all-gather.2
where the time goes:
time: 271 us
  waiting for transfers between devices  192 us (71%)
  blocking collectives  38.2 us (14%)
  between operations  14.1 us (5%)
  matrix products  11.4 us (4%)
  starting transfers between devices  10.4 us (4%)
  local copies, waits for them, and re-layouts  2.8 us (1%)
    all_gather x1, waiting for transfers between devices, body(): lax.all_gather(weight, 'tok', axis=0, tiled=True)  108 us
    all_gather x1, waiting for transfers between devices, body(): features = lax.all_gather(hidden, 'vocab', axis=1, tiled=True)  67.4 us
    psum x1, blocking collectives, body(): lax.psum((domain_sum, domain_count), ('tok', 'vocab'))  38.2 us
    dot_general x1, matrix products, body(): jnp.dot(features, lax.all_gather(weight, 'tok', axis=0, tiled=True), pref...  11.1 us
    all_to_all x1, waiting for transfers between devices, body(): lax.all_to_all(sum_loc.reshape(groups, share_len), 'vocab', split_axis=0,...  6.14 us
  transfers between devices with their start and end apart: 5, of which 5 were waited for; matrix products, arithmetic and copies ran while one was open for 1% of the time, Pallas kernels for 0%

commit v1 on v0

--- a/solution.py
+++ b/solution.py
@@ -11,11 +11,14 @@
     features = lax.all_gather(hidden, "vocab", axis=1, tiled=True)
     tok_rows = features.shape[0]
     columns = weight.shape[1]
-    logits = jnp.dot(
-        features,
-        lax.all_gather(weight, "tok", axis=0, tiled=True),
-        preferred_element_type=jnp.float32,
-    )
+
+    def layers_all_rest(local_x, bus_axis):
+        mid_arr = jnp.concatenate(
+            [local_x, lax.ppermute(local_x, axis_name=bus_axis, perm=[(0, 1), (1, 0)])], axis=0
+        )
+        return jnp.roll(mid_arr, lax.axis_index(bus_axis) * local_x.shape[0], 0)
+
+    logits = jnp.dot(features, layers_all_rest(weight, "tok"), preferred_element_type=jnp.float32)
     first_col = lax.axis_index("vocab") * columns
     column_ids = first_col + lax.broadcasted_iota(jnp.int32, (tok_rows, columns), 1)
     picked_loc = jnp.sum(jnp.where(column_ids == targets[:, None], logits, 0.0), axis=1)

time: 271 us -> 199 us (0.73)
  waiting for transfers between devices: 192 us -> 108 us
  matrix products: 11.4 us -> 18.3 us
  starting transfers between devices: 10.4 us -> 16.2 us
    all_gather x1 -> x0, waiting for transfers between devices: 108 us -> none  [body(): lax.all_gather(weight, 'tok', axis=0, tiled=True)]
    ppermute x0 -> x1, waiting for transfers between devices: none -> 90.8 us  [layers_all_rest(): lax.ppermute(local_x, axis_name=bus_axis, perm=[(0, 1), (1, 0)])]
    all_gather x1, waiting for transfers between devices: 67.4 us -> 0.01 us  [body(): features = lax.all_gather(hidden, 'vocab', axis=1, tiled=True)]
    dot_general x1, matrix products: 11.1 us -> 17.9 us  [body(): jnp.dot(features, layers_all_rest(weight, 'tok'), preferred_element_type=...]
    ppermute x0 -> x1, starting transfers between devices: none -> 3.03 us  [layers_all_rest(): lax.ppermute(local_x, axis_name=bus_axis, perm=[(0, 1), (1, 0)])]
    all_to_all x1, starting transfers between devices: 3.41 us -> 6.18 us  [body(): lax.all_to_all(top_loc.reshape(groups, share_len), 'vocab', split_axis=0,...]
  transfers between devices with their start and end apart: 5 -> 5, of which waited for: 5 -> 4; matrix products, arithmetic and copies ran while one was open for 1% -> 1% of each run, Pallas kernels for 0% -> 0%
where the time goes in v1:
time: 199 us; the launch traced here: 198 us
  waiting for transfers between devices  108 us (54%)
  blocking collectives  38.2 us (19%)
  matrix products  18.3 us (9%)
  starting transfers between devices  16.2 us (8%)
  between operations  14.1 us (7%)
  local copies, waits for them, and re-layouts  2.8 us (1%)
    ppermute x1, waiting for transfers between devices, layers_all_rest(): lax.ppermute(local_x, axis_name=bus_axis, perm=[(0, 1), (1, 0)])  90.8 us
    psum x1, blocking collectives, body(): lax.psum((domain_sum, domain_count), ('tok', 'vocab'))  38.2 us
    dot_general x1, matrix products, body(): jnp.dot(features, layers_all_rest(weight, 'tok'), preferred_element_type=...  17.9 us
    all_to_all x1, starting transfers between devices, body(): lax.all_to_all(top_loc.reshape(groups, share_len), 'vocab', split_axis=0,...  6.18 us
    all_to_all x1, waiting for transfers between devices, body(): lax.all_to_all(sum_loc.reshape(groups, share_len), 'vocab', split_axis=0,...  6.14 us
    all_to_all x1, waiting for transfers between devices, body(): lax.all_to_all(top_loc.reshape(groups, share_len), 'vocab', split_axis=0,...  4.99 us
    all_to_all x1, waiting for transfers between devices, body(): lax.all_to_all(picked_loc.reshape(groups, share_len), 'vocab', split_axis...  4.87 us
  transfers between devices with their start and end apart: 5, of which 4 were waited for; matrix products, arithmetic and copies ran while one was open for 1% of the time, Pallas kernels for 0%

profile of v1, /device:TPU:0, one launch (start us, length us, event | category | flops | bytes accessed | tf_op | source)
XLA Modules:
  0.0 198.5 jit_solution(5273640786038862610)
XLA Ops:
  7.2 0.0 all-gather.2.cloned.1.call-start
  7.2 0.7 all-gather.2.cloned.1.call-update
  7.9 3.0 %collective-permute-start = (bf16[2048,1024]{1,0:T(8,128)(2,1)}, bf16[2048,1024]{1,0:T(8,128)(2,1)}, u32[]{:S(2)}, u32[]{:S(2)}) collective-permute-start(bf16[2048,1024]{1,0:T(8,128)(2,1)} %param.6), channel_id=1, source_target_pairs={{0,16},{16,0},{1,17},{17,1},{2,18},{18,2},{3,19},{19,3},{4,20},{20... | collective-permute-start | bytes 12582920 | tf_op jit(solution)/shard_map/ppermute | solution.py:17
  11.0 0.0 copy-start
  11.0 0.0 copy-start.2
  11.0 90.8 %collective-permute-done = bf16[2048,1024]{1,0:T(8,128)(2,1)} collective-permute-done((bf16[2048,1024]{1,0:T(8,128)(2,1)}, bf16[2048,1024]{1,0:T(8,128)(2,1)}, u32[]{:S(2)}, u32[]{:S(2)}) %collective-permute-start) | collective-permute-done | bytes 4194336 | tf_op jit(solution)/shard_map/ppermute | solution.py:17
  101.8 0.0 all-gather.2.cloned.1.call-done
  101.8 17.9 %fusion.16 = (f32[768]{0:T(1024)S(1)}, f32[1024,768]{1,0:T(8,128)S(1)}) fusion(bf16[768,4096]{1,0:T(8,128)(2,1)} %all-gather.2.cloned.1.call-done, s32[]{:T(128)S(6)} %select_n.43, bf16[2048,1024]{1,0:T(8,128)(2,1)} %param.6, bf16[2048,1024]{1,0:T(8,128)(2,1)} %collective-permute-done), kind=kOutput, calls=%fused_computation.35 | convolution fusion | flops 6476790784 | bytes 17828868 | tf_op jit(solution)/shard_map/dot_general | solution.py:21
  119.7 0.7 all_to_all.25
  120.4 6.2 %all-to-all-start.1 = ((f32[16,1,48]{2,1,0:T(1,128)}), f32[16,1,48]{2,1,0:T(1,128)S(1)}, u32[]{:S(2)}, u32[]{:S(2)}) async-start(f32[16,1,48]{2,1,0:T(1,128)} %all_to_all.25), calls=%async_computation.1 | async-start | bytes 16384 | tf_op jit(solution)/shard_map/all_to_all | solution.py:31
  126.6 0.0 copy-done
  126.6 0.7 fusion.6
  127.3 0.7 all_to_all.28
  128.0 5.0 %all-to-all-done.1 = f32[16,1,48]{2,1,0:T(1,128)S(1)} async-done(((f32[16,1,48]{2,1,0:T(1,128)}), f32[16,1,48]{2,1,0:T(1,128)S(1)}, u32[]{:S(2)}, u32[]{:S(2)}) %all-to-all-start.1) | async-done | bytes 3104 | tf_op jit(solution)/shard_map/all_to_all | solution.py:31
  133.0 3.5 %all-to-all-start.2 = ((f32[16,1,48]{2,1,0:T(1,128)}), f32[16,1,48]{2,1,0:T(1,128)S(1)}, u32[]{:S(2)}, u32[]{:S(2)}) async-start(f32[16,1,48]{2,1,0:T(1,128)} %all_to_all.28), calls=%async_computation.2 | async-start | bytes 16384 | tf_op jit(solution)/shard_map/all_to_all | solution.py:37
  136.5 0.0 copy-done.2
  136.5 0.1 select_reduce_fusion
  136.6 0.8 dynamic_slice.8
  137.4 0.7 all_to_all.22
  138.0 4.9 %all-to-all-done.2 = f32[16,1,48]{2,1,0:T(1,128)S(1)} async-done(((f32[16,1,48]{2,1,0:T(1,128)}), f32[16,1,48]{2,1,0:T(1,128)S(1)}, u32[]{:S(2)}, u32[]{:S(2)}) %all-to-all-start.2) | async-done | bytes 3104 | tf_op jit(solution)/shard_map/all_to_all | solution.py:37
  142.9 3.4 %all-to-all-start = ((f32[16,1,48]{2,1,0:T(1,128)}), f32[16,1,48]{2,1,0:T(1,128)S(1)}, u32[]{:S(2)}, u32[]{:S(2)}) async-start(f32[16,1,48]{2,1,0:T(1,128)} %all_to_all.22), calls=%async_computation | async-start | bytes 16384 | tf_op jit(solution)/shard_map/all_to_all | solution.py:34
  146.3 0.2 convolution_bitcast_fusion
  146.6 6.1 %all-to-all-done = f32[16,1,48]{2,1,0:T(1,128)S(1)} async-done(((f32[16,1,48]{2,1,0:T(1,128)}), f32[16,1,48]{2,1,0:T(1,128)S(1)}, u32[]{:S(2)}, u32[]{:S(2)}) %all-to-all-start) | async-done | bytes 3104 | tf_op jit(solution)/shard_map/all_to_all | solution.py:34
  152.7 0.0 copy-start.1
  152.8 0.2 convolution_bitcast_fusion.1
  153.0 38.2 %all-reduce = (f32[64]{0:T(128)S(1)}, f32[64]{0:T(128)S(1)}) all-reduce(f32[64]{0:T(128)S(1)} %convolution_bitcast_fusion.1, f32[64]{0:T(128)S(1)} %convolution_bitcast_fusion), channel_id=1, replica_groups=mesh['tok'=2,'vocab'=16] {'tok','vocab'}, use_global_device_ids=true, to_apply=%region_7.8 | all-reduce | flops 128 | bytes 1024 | tf_op jit(solution)/shard_map/psum | solution.py:64
  191.1 0.5 maximum_divide_fusion
  191.6 0.0 copy-done.1
  (6 shorter events, 0.1 us)
Async XLA Ops:
  7.2 94.7 %all-gather.2.cloned.1.call-start = ((), (), s32[]{:S(2)}) async-start(), calls=%async_computation.3 | async-start | bytes 6684672 | tf_op jit(solution)/shard_map/all_gather | solution.py:11
  7.9 93.9 %collective-permute-start = (bf16[2048,1024]{1,0:T(8,128)(2,1)}, bf16[2048,1024]{1,0:T(8,128)(2,1)}, u32[]{:S(2)}, u32[]{:S(2)}) collective-permute-start(bf16[2048,1024]{1,0:T(8,128)(2,1)} %param.6), channel_id=1, source_target_pairs={{0,16},{16,0},{1,17},{17,1},{2,18},{18,2},{3,19},{19,3},{4,20},{20... | collective-permute-start | bytes 12582920 | tf_op jit(solution)/shard_map/ppermute | solution.py:17
  11.0 115.6 %copy-start = (s32[768]{0:T(1024)S(1)}, s32[768]{0:T(1024)}, u32[]{:S(2)}) copy-start(s32[768]{0:T(1024)} %param.7) | copy-start | bytes 9220
  11.0 125.5 %copy-start.2 = (s32[6]{0:T(128)S(1)}, s32[6]{0:T(128)}, u32[]{:S(2)}) copy-start(s32[6]{0:T(128)} %param.9) | copy-start | bytes 76
  120.4 12.6 %all-to-all-start.1 = ((f32[16,1,48]{2,1,0:T(1,128)}), f32[16,1,48]{2,1,0:T(1,128)S(1)}, u32[]{:S(2)}, u32[]{:S(2)}) async-start(f32[16,1,48]{2,1,0:T(1,128)} %all_to_all.25), calls=%async_computation.1 | async-start | bytes 16384 | tf_op jit(solution)/shard_map/all_to_all | solution.py:31
  133.0 9.9 %all-to-all-start.2 = ((f32[16,1,48]{2,1,0:T(1,128)}), f32[16,1,48]{2,1,0:T(1,128)S(1)}, u32[]{:S(2)}, u32[]{:S(2)}) async-start(f32[16,1,48]{2,1,0:T(1,128)} %all_to_all.28), calls=%async_computation.2 | async-start | bytes 16384 | tf_op jit(solution)/shard_map/all_to_all | solution.py:37
  142.9 9.8 %all-to-all-start = ((f32[16,1,48]{2,1,0:T(1,128)}), f32[16,1,48]{2,1,0:T(1,128)S(1)}, u32[]{:S(2)}, u32[]{:S(2)}) async-start(f32[16,1,48]{2,1,0:T(1,128)} %all_to_all.22), calls=%async_computation | async-start | bytes 16384 | tf_op jit(solution)/shard_map/all_to_all | solution.py:34
  152.7 38.9 %copy-start.1 = (f32[48]{0:T(128)}, f32[48]{0:T(128)S(1)}, u32[]{:S(2)}) copy-start(f32[48]{0:T(128)S(1)} %subtract_select_fusion) | copy-start | bytes 580
Sparse Core Ops, SparseCore 0:
  10.1 67.9 all-gather.1
